TPU v7x, 32 devices: a whole 2x2x4 slice. The times are simulated.
32 devices in a mesh: row: 2 (over y), phi: 16 (over z, x, core).
Axes of the slice: x: 2, y: 2, z: 4, core: 2. Of those that a mesh axis runs over, the one named last changes fastest.
Arguments:
- density: float32 [32, 2048, 512], P('row', 'phi'), may hold values from 0.3 to 3
- velocity: float32 [3, 32, 2048, 512], P(None, 'row', 'phi'), may hold values from -3 to 3
- magnetic: float32 [3, 32, 2048, 512], P(None, 'row', 'phi'), may hold values from -6 to 6
Outputs:
- density_next: float32 [32, 2048, 512], P('row', 'phi')
- magnetic_next: float32 [3, 32, 2048, 512], P(None, 'row', 'phi')
All inputs are finite; a program needn't handle non-finite values.
Results may differ from a plain program's by a relative error of at most 0.0003.
Values sent between devices are 32-bit elements; how exact they have to be, the bound alone decides.
A program may use at most 256 MiB of HBM per device.

v0:
```python
import math

import jax
import jax.numpy as jnp
import numpy as np
from jax import lax
from jax.experimental import pallas as pl
from jax.experimental.pallas import tpu as pltpu
from jax.sharding import PartitionSpec as P


NPOL = 128
RADIX = 16
FRONT = 16
TILE = 8
HALO = 8
REACH = 3

COURANT_RAD = 0.3
COURANT_POL = 0.25
COURANT_AZI = 0.35
SOUND_SPEED = 1.0


def rotate(value, angle):
    re, im = value
    c, s = math.cos(angle), math.sin(angle)
    if im is None:
        return (re * c, re * s)
    return (re * c - im * s, re * s + im * c)


def add(a, b, sign=1.0):
    def part(x, y):
        if y is None:
            return x
        if x is None:
            return y if sign > 0 else -y
        return x + y if sign > 0 else x - y

    return (part(a[0], b[0]), part(a[1], b[1]))


def conj(a):
    return (a[0], None if a[1] is None else -a[1])


def real_fft(xs):
    n = len(xs)
    if n == 1:
        return [(xs[0], None)]
    if n == 2:
        return [(xs[0] + xs[1], None), (xs[0] - xs[1], None)]
    even, odd = real_fft(xs[0::2]), real_fft(xs[1::2])
    half = n // 2

    def at(spec, k):
        return spec[k] if k <= half // 2 else conj(spec[half - k])

    result = []
    for k in range(half + 1):
        e, o = at(even, k % half), at(odd, k % half)
        if k == 0:
            result.append(add(e, o))
        elif k == half:
            result.append(add(e, o, -1.0))
        elif 4 * k == n:
            result.append((e[0], -o[0]))
        else:
            result.append(add(e, rotate(o, -2.0 * math.pi * k / n)))
    return result


def real_ifft(spec, n):
    if n == 2:
        a, b = spec[0][0], spec[1][0]
        return [a + b, a - b]
    half = n // 2
    even, odd = [], []
    for k in range(half // 2 + 1):
        a, b = spec[k], conj(spec[half - k])
        if k == 0:
            a, b = (spec[0][0], None), (spec[half][0], None)
            even.append(add(a, b))
            odd.append(add(a, b, -1.0))
        elif 4 * k == n:
            even.append((2.0 * spec[k][0], None))
            odd.append((-2.0 * spec[k][1], None))
        else:
            even.append(add(a, b))
            odd.append(rotate(add(a, b, -1.0), 2.0 * math.pi * k / n))
    evens, odds = real_ifft(even, half), real_ifft(odd, half)
    return [v for pair in zip(evens, odds) for v in pair]


def filter_tables(cells, theta_count):
    inner = cells // RADIX
    half_polar = NPOL // 2
    k2 = np.arange(RADIX // 2 + 1)[:, None]
    mode = k2 + RADIX * np.arange(inner)[None, :]
    angle = 2.0 * np.pi / cells * ((mode[:, :, None] * np.arange(inner)) % cells)
    cos, sin = np.cos(angle), np.sin(angle)
    forward = np.concatenate(
        [np.concatenate([cos, sin], 2), np.concatenate([-sin, cos], 2)], 1
    ).astype(np.float32)
    rows = np.arange(NPOL)
    theta = np.where(rows < half_polar, rows, theta_count - NPOL + rows)
    row_square = np.sin(np.pi * (theta + 0.5) / theta_count) ** 2
    edge = np.sin(np.pi * (half_polar + 0.5) / theta_count)
    mode_square = (edge * np.sin(np.pi * mode / cells)) ** 2
    damping = row_square / np.maximum(row_square, mode_square[:, :, None])
    return forward, (damping / cells).astype(np.float32)


def filter_kernel(group, inner, blocks, *refs):
    x_refs = refs[:group]
    basis_ref, damp_ref, out_ref = refs[group:]
    devices, _, azimuth, _ = x_refs[0].shape

    def slab(d):
        parts = [
            x_refs[g][d * blocks : (d + 1) * blocks, 0].reshape(inner, NPOL) for g in range(group)
        ]
        return jnp.concatenate(parts, axis=1) if group > 1 else parts[0]

    spectrum = real_fft([slab(d) for d in range(RADIX)])
    filtered = []
    for k, (re, im) in enumerate(spectrum):
        basis = basis_ref[k]
        if im is None:
            forward = basis[:, :inner]
            stacked = re
        else:
            forward = basis
            stacked = jnp.concatenate([re, im], axis=0)
        modes = jnp.dot(
            forward, stacked, precision=lax.Precision.HIGHEST, preferred_element_type=jnp.float32
        )
        damp = damp_ref[k]
        damp = jnp.concatenate([damp, damp], axis=0)
        if group > 1:
            damp = jnp.concatenate([damp] * group, axis=1)
        back = lax.dot_general(
            forward,
            modes * damp,
            (((0,), (0,)), ((), ())),
            precision=lax.Precision.HIGHEST,
            preferred_element_type=jnp.float32,
        )
        filtered.append((back, None) if im is None else (back[:inner], back[inner:]))
    for d, value in enumerate(real_ifft(filtered, RADIX)):
        for g in range(group):
            out_ref[d * blocks : (d + 1) * blocks, g, :azimuth] = value[
                :, g * NPOL : (g + 1) * NPOL
            ].reshape(blocks, azimuth, NPOL)
    blank = jnp.zeros((HALO - 2 * REACH, NPOL), jnp.float32)
    for d in range(devices):
        for g in range(group):
            below = out_ref[(d - 1) % devices, g, azimuth - REACH : azimuth]
            above = out_ref[(d + 1) % devices, g, :REACH]
            out_ref[d, g, azimuth:] = jnp.concatenate([below, above, blank], axis=0)


def filter_lines(lines, first, group, theta_count):
    devices, _, azimuth, _ = lines.shape
    cells = devices * azimuth
    inner = cells // RADIX
    blocks = inner // azimuth
    forward, damping = filter_tables(cells, theta_count)

    def slot(g):
        return pl.BlockSpec((devices, 1, azimuth, NPOL), lambda p: (0, first + g, 0, 0))

    shape = (devices, group, azimuth + HALO, NPOL)
    return pl.pallas_call(
        lambda *refs: filter_kernel(group, inner, blocks, *refs),
        grid=(1,),
        in_specs=[slot(g) for g in range(group)]
        + [
            pl.BlockSpec(forward.shape, lambda p: (0, 0, 0)),
            pl.BlockSpec(damping.shape, lambda p: (0, 0, 0)),
        ],
        out_specs=pl.BlockSpec(shape, lambda p: (0, 0, 0, 0)),
        out_shape=jax.ShapeDtypeStruct(shape, jnp.float32),
        compiler_params=pltpu.CompilerParams(vmem_limit_bytes=56 * 1024 * 1024),
        cost_estimate=pl.CostEstimate(
            flops=32 * inner * cells * NPOL * group, bytes_accessed=8 * lines.size, transcendentals=0
        ),
        name="polar_filter",
    )(*[lines] * group, jnp.asarray(forward), jnp.asarray(damping))


def pack_lines(density, velocity, order, first, slots, depth):
    _, azimuth, width = density.shape
    half = NPOL // 2
    last = width // NPOL - 1

    def kernel(order, d0, d1, v0, v1, out):
        lane = lax.broadcasted_iota(jnp.int32, (azimuth, NPOL), 1)
        for i in range(depth):
            out[0, i, 0] = jnp.where(lane < half, d0[i], d1[i])
            for c in range(3):
                out[1 + c, i, 0] = jnp.where(lane < half, v0[c, i], v1[c, i])

    def block(t, s):
        return s[0] + (first + t) * s[1]

    def dens(tile):
        return pl.BlockSpec((depth, azimuth, NPOL), lambda t, s: (block(t, s), 0, tile))

    def vel(tile):
        return pl.BlockSpec((3, depth, azimuth, NPOL), lambda t, s: (0, block(t, s), 0, tile))

    return pl.pallas_call(
        kernel,
        grid_spec=pltpu.PrefetchScalarGridSpec(
            num_scalar_prefetch=1,
            grid=(slots,),
            in_specs=[dens(0), dens(last), vel(0), vel(last)],
            out_specs=pl.BlockSpec((4, depth, 1, azimuth, NPOL), lambda t, s: (0, 0, t, 0, 0)),
        ),
        out_shape=jax.ShapeDtypeStruct((4, depth, slots, azimuth, NPOL), jnp.float32),
        name="pack_lines",
    )(order, density, density, velocity, velocity)


def pack_sides(density, velocity, magnetic):
    radial, azimuth, width = density.shape
    last = azimuth // TILE - 1
    step = 4 if radial % 4 == 0 else 1

    def kernel(d0, d1, v0, v1, m0, m1, low, high):
        def rows(i, dens, vel, mag, pick, wide):
            parts = [dens[i, pick(REACH)], vel[2, i, pick(REACH)], vel[0, i, pick(1)], vel[1, i, pick(1)]]
            parts += [mag[0, i, pick(1)], mag[1, i, pick(1)], mag[2, i, pick(wide)]]
            used = sum(p.shape[0] for p in parts)
            parts.append(jnp.zeros((PACKED - used, width), jnp.float32))
            return jnp.concatenate(parts, axis=0)

        for i in range(step):
            low[i] = rows(i, d0, v0, m0, lambda n: slice(0, n), 2)
            high[i] = rows(i, d1, v1, m1, lambda n: slice(TILE - n, TILE), 1)

    def three(b):
        return pl.BlockSpec((3, step, TILE, width), lambda t: (0, t, b, 0))

    def one(b):
        return pl.BlockSpec((step, TILE, width), lambda t: (t, b, 0))

    return pl.pallas_call(
        kernel,
        grid=(radial // step,),
        in_specs=[one(0), one(last), three(0), three(last), three(0), three(last)],
        out_specs=[pl.BlockSpec((step, PACKED, width), lambda t: (t, 0, 0))] * 2,
        out_shape=[jax.ShapeDtypeStruct((radial, PACKED, width), jnp.float32)] * 2,
        name="pack_sides",
    )(density, density, velocity, velocity, magnetic, magnetic)


def interface_value(outer_left, inner_left, inner_right, outer_right):
    guess = 7.0 / 12.0 * (inner_left + inner_right) - 1.0 / 12.0 * (outer_left + outer_right)
    low = jnp.minimum(inner_left, inner_right)
    return jnp.minimum(jnp.maximum(guess, low), jnp.maximum(inner_left, inner_right))


def limited(centre, left_face, right_face):
    to_left = left_face - centre
    to_right = right_face - centre
    reach_right = 2.0 * jnp.abs(to_right)
    reach_left = 2.0 * jnp.abs(to_left)
    left = jnp.minimum(jnp.maximum(to_left, -reach_right), reach_right)
    right = jnp.minimum(jnp.maximum(to_right, -reach_left), reach_left)
    return centre + left, centre + right


def hll_flux(dens_left, dens_right, speed_left, speed_right):
    slowest = jnp.minimum(jnp.minimum(speed_left, speed_right) - SOUND_SPEED, 0.0)
    fastest = jnp.maximum(jnp.maximum(speed_left, speed_right) + SOUND_SPEED, 0.0)
    from_left = fastest * dens_left * (speed_left - slowest)
    from_right = slowest * dens_right * (speed_right - fastest)
    return (from_left - from_right) / (fastest - slowest)


PRIM_ROWS = ((0, 0, 3), (3, 3, 3), (1, 6, 1), (2, 7, 1))
MAG_ROWS_LOW = ((4, 8, 1), (5, 9, 1), (6, 10, 1))
MAG_ROWS_HIGH = ((4, 8, 1), (5, 9, 1), (6, 10, 2))
PACKED = 16


def stencil_kernel(middle, radial, azimuth, parts, starts, refs, ghosts, outs, scratch):
    (s0, s1, s2, s3, s4, s5, s6, er, et, ep) = scratch[:10]
    carry_rho, carry_u, carry_flux, face_of_rho, face_of_u = scratch[10:]
    state = (s0, s1, s2, s3, s4, s5, s6)
    t = pl.program_id(0)
    width = s0.shape[-1]
    half = NPOL // 2
    slot = lax.rem(t, 8)
    layer = starts[0] + t - 3
    own = slice(FRONT, FRONT + azimuth)
    dens_out, mag_out = outs

    def low_lanes(rows):
        return lax.broadcasted_iota(jnp.int32, (rows, NPOL), 1) < half

    def ring(x):
        full = x.shape[1]
        mixed = jnp.where(low_lanes(x.shape[0]), x[:, full - NPOL :], x[:, :NPOL])
        return jnp.concatenate([x[:, NPOL : full - NPOL], mixed], axis=1)

    def outer(x, pol=None):
        lanes = low_lanes(x.shape[0])
        a, b = x[:, :NPOL], x[:, x.shape[1] - NPOL :]
        if pol is not None:
            a, b = jnp.where(lanes, pol, a), jnp.where(lanes, b, pol)
        return jnp.concatenate([a, b], axis=1)

    edge = azimuth + REACH

    def fill(fields, pols, low, high):
        for f, x in enumerate(fields):
            if middle:
                state[f][slot, own] = ring(x())
            elif f < 4:
                state[f][slot, own] = outer(x(), pols[f][:azimuth])
            else:
                state[f][slot, own] = outer(x())
        for f, row, n in PRIM_ROWS:
            a, b = low[row : row + n], high[row : row + n]
            if middle:
                a, b = ring(a), ring(b)
            else:
                a = outer(a, pols[f][edge - n : edge])
                b = outer(b, pols[f][edge : edge + n])
            state[f][slot, FRONT - n : FRONT] = a
            state[f][slot, FRONT + azimuth : FRONT + azimuth + n] = b
        shape = ring if middle else outer
        for f, row, n in MAG_ROWS_LOW:
            state[f][slot, FRONT - n : FRONT] = shape(low[row : row + n])
        for f, row, n in MAG_ROWS_HIGH:
            state[f][slot, FRONT + azimuth : FRONT + azimuth + n] = shape(high[row : row + n])

    mid_dens = mid_mag = None
    if middle:
        dens, vel, mag, side_low, side_high = refs
        fields = [lambda: dens[0]]
        fields += [lambda c=c: vel[c, 0] for c in range(3)]
        fields += [lambda c=c: mag[c, 0] for c in range(3)]
        choices = [(None, None)]
    else:
        d0, d1, v0, v1, m0, m1, pols, side_low, side_high, mid_dens, mid_mag = refs

        def both(a, b):
            return jnp.concatenate([a, b], axis=1)

        fields = [lambda: both(d0[0], d1[0])]
        fields += [lambda c=c: both(v0[c, 0], v1[c, 0]) for c in range(3)]
        fields += [lambda c=c: both(m0[c, 0], m1[c, 0]) for c in range(3)]
        choices = []
        for (first, slots, depth), pol in zip(parts, pols):
            inside = None
            if len(pols) > 1:
                block = jnp.clip(layer, 0, radial - 1) // depth
                place = (block - starts[2]) * starts[3] - first
                inside = (place >= 0) & (place < slots)
            choices.append((pol, inside))
    mine = None if ghosts is None else (layer >= 0) & (layer < radial)
    for pol, inside in choices:
        def load(pol=pol):
            pieces = None if pol is None else [pol.at[c, 0, 0] for c in range(4)]
            fill(fields, pieces, side_low.at[0], side_high.at[0])

        cond = mine if inside is None else inside if mine is None else mine & inside
        if cond is None:
            load()
        else:
            pl.when(cond)(load)
    if ghosts is not None:
        @pl.when(jnp.logical_not(mine))
        def _():
            planes = [lambda r=r: r[0] for r in ghosts[:7]]
            pieces = [r.at[0] for r in ghosts[9:]]
            fill(planes, pieces, ghosts[7].at[0], ghosts[8].at[0])

    shape = (TILE, width)
    lane = lax.broadcasted_iota(jnp.int32, shape, 1)
    sub = lax.broadcasted_iota(jnp.int32, shape, 0)

    def shifted(ref, index, base, off):
        here = ref[index, pl.ds(base, TILE), :]
        if off > 0:
            other = ref[index, pl.ds(base + TILE, TILE), :]
            return pltpu.roll(jnp.where(sub < off, other, here), TILE - off, 0)
        if off < 0:
            other = ref[index, pl.ds(base - TILE, TILE), :]
            return pltpu.roll(jnp.where(sub >= TILE + off, other, here), -off, 0)
        return here

    def at(ref, d, base, off=0):
        return shifted(ref, lax.rem(t - 3 + d + 8, 8), base, off)

    def up(x):
        rolled = pltpu.roll(x, width - 1, 1)
        return rolled if middle else jnp.where(lane == width - 1, x, rolled)

    def down(x):
        rolled = pltpu.roll(x, 1, 1)
        return rolled if middle else jnp.where(lane == 0, x, rolled)

    def before(x, previous):
        return jnp.where(sub == 0, pltpu.roll(previous, 1, 0), pltpu.roll(x, 1, 0))

    def azimuth_step(base, carry):
        rights, lefts, kept = [], [], []
        for field, past_face, past_right in ((s0, carry[0], carry[2]), (s3, carry[1], carry[3])):
            q = [at(field, 0, base, o) for o in (-1, 0, 1, 2)]
            face = interface_value(*q)
            left, right = limited(q[1], before(face, past_face), face)
            rights.append(before(right, past_right))
            lefts.append(left)
            kept.append((face, right))
        flux = hll_flux(rights[0], lefts[0], rights[1], lefts[1])
        return (kept[0][0], kept[1][0], kept[0][1], kept[1][1]), flux

    def theta_edges(q):
        below = down(q)
        face = interface_value(down(below), below, q, up(q))
        rolled = pltpu.roll(face, width - 1, 1)
        above = rolled if middle else jnp.where(lane == width - 1, q, rolled)
        return limited(q, face, above)

    here = lax.rem(t, 4)

    def emf_tile(j, _):
        base = pl.multiple_of(FRONT - TILE + j * TILE, TILE)
        u_r, u_t, u_p = (at(s, 1, base) for s in (s1, s2, s3))
        b_r = at(s4, 1, base) + at(s4, 2, base)
        b_t = at(s5, 1, base)
        b_t = b_t + up(b_t)
        b_p = at(s6, 1, base) + at(s6, 1, base, 1)
        rows = pl.ds(base, TILE)
        er[here, rows, :] = u_p * b_t - u_t * b_p
        et[here, rows, :] = u_r * b_p - u_p * b_r
        ep[here, rows, :] = u_t * b_r - u_r * b_t
        return 0

    @pl.when(t >= 4)
    def _():
        lax.fori_loop(0, azimuth // TILE + 2, emf_tile, 0, unroll=math.gcd(azimuth // TILE + 2, 6))

    def emf(ref, d, base, off=0):
        return shifted(ref, lax.rem(t - 1 + d + 4, 4), base, off)

    def radial_face(field, base):
        return interface_value(*(at(field, d, base) for d in (0, 1, 2, 3)))

    def radial_step(rows, base):
        face_rho, face_u = radial_face(s0, base), radial_face(s1, base)
        left_r, right_r = limited(at(s0, 1, base), face_of_rho[rows, :], face_rho)
        left_u, right_v = limited(at(s1, 1, base), face_of_u[rows, :], face_u)
        flux = hll_flux(carry_rho[rows, :], left_r, carry_u[rows, :], left_u)
        total = COURANT_RAD * (flux - carry_flux[rows, :])
        face_of_rho[rows, :] = face_rho
        face_of_u[rows, :] = face_u
        carry_rho[rows, :] = right_r
        carry_u[rows, :] = right_v
        carry_flux[rows, :] = flux
        return total

    def put(ref, index, rows, value, mid):
        if middle:
            ref[index + (rows, slice(None))] = value
            return
        inner = width + NPOL
        keep = lax.broadcasted_iota(jnp.int32, (TILE, NPOL), 1)
        mixed = mid[:, inner - NPOL :]
        quarter = half // 2
        first = jnp.where(keep < half + quarter, value[:, :NPOL], mixed)
        last = jnp.where(keep >= quarter, value[:, NPOL:], mixed)
        ref[index + (rows, slice(0, NPOL))] = first
        ref[index + (rows, slice(NPOL, inner))] = mid[:, : inner - NPOL]
        ref[index + (rows, slice(inner, inner + NPOL))] = last

    def middle_of(rows, c=None):
        if middle:
            return None
        return mid_dens[0, rows, :] if c is None else mid_mag[c, 0, rows, :]

    def tile(j, carry):
        kept, flux_low = carry
        start = pl.multiple_of(j * TILE, TILE)
        base = pl.multiple_of(FRONT + j * TILE, TILE)
        rows = pl.ds(start, TILE)

        total = radial_step(rows, base)

        kept, flux = azimuth_step(base + TILE, kept)
        flux_high = pltpu.roll(jnp.where(sub < 1, flux, flux_low), TILE - 1, 0)
        total = total + COURANT_AZI * (flux_high - flux_low)
        flux_low = flux

        rho = at(s0, 0, base)
        left_r, right_r = theta_edges(rho)
        left_u, right_v = theta_edges(at(s2, 0, base))
        theta_flux = hll_flux(down(right_r), left_r, down(right_v), left_u)
        if not middle:
            theta_flux = jnp.where(lane == 0, 0.0, theta_flux)
        above = pltpu.roll(theta_flux, width - 1, 1)
        if not middle:
            above = jnp.where(lane == width - 1, 0.0, above)
        total = total + COURANT_POL * (above - theta_flux)
        put(dens_out, (0,), rows, rho - total, middle_of(rows))

        er_low, er_here, er_high = (emf(er, 0, base, o) for o in (-1, 0, 1))
        ep_low, ep_here, ep_high = (emf(ep, d, base) for d in (-1, 0, 1))
        below_k = emf(et, -1, base, -1)
        edge_a = ep_low + ep_here
        edge_r = er_low + er_here
        mixed = (0.125 * COURANT_RAD) * (ep_high - ep_low) - (0.125 * COURANT_AZI) * (er_high - er_low)
        across = emf(et, -1, base, 1) + emf(et, 0, base, 1) - below_k - emf(et, 0, base, -1)
        along = emf(et, 1, base, -1) + emf(et, 1, base) - below_k - emf(et, -1, base)
        put(mag_out, (0, 0), rows,
            at(s4, 0, base)
            - (0.125 * COURANT_POL) * (up(edge_a) - down(edge_a))
            + (0.125 * COURANT_AZI) * across, middle_of(rows, 0))
        put(mag_out, (1, 0), rows, at(s5, 0, base) + (down(mixed) + mixed), middle_of(rows, 1))
        put(mag_out, (2, 0), rows,
            at(s6, 0, base)
            - (0.125 * COURANT_RAD) * along
            + (0.125 * COURANT_POL) * (up(edge_r) - down(edge_r)), middle_of(rows, 2))
        return kept, flux_low

    @pl.when(t == 3)
    def _():
        def warm_face(j, _):
            rows = pl.ds(pl.multiple_of(j * TILE, TILE), TILE)
            base = pl.multiple_of(FRONT + j * TILE, TILE)
            face_of_rho[rows, :] = radial_face(s0, base)
            face_of_u[rows, :] = radial_face(s1, base)
            return 0

        lax.fori_loop(0, azimuth // TILE, warm_face, 0, unroll=2)

    @pl.when((t >= 4) & (t < 6))
    def _():
        def warm(j, _):
            start = pl.multiple_of(j * TILE, TILE)
            radial_step(pl.ds(start, TILE), pl.multiple_of(FRONT + j * TILE, TILE))
            return 0

        lax.fori_loop(0, azimuth // TILE, warm, 0, unroll=2)

    @pl.when(t >= 6)
    def _():
        zero = jnp.zeros(shape, jnp.float32)
        kept, _ = azimuth_step(FRONT - TILE, (zero, zero, zero, zero))
        first = azimuth_step(FRONT, kept)
        unroll = math.gcd(azimuth // TILE, 4 if middle else 8)
        lax.fori_loop(0, azimuth // TILE, tile, first, unroll=unroll)


def stencil(middle, count, starts, fields, sides, ghosts=None, polar=None, mids=None, into=None):
    density, velocity, magnetic = fields
    radial, azimuth, width = density.shape
    tiles = width // NPOL

    def own(t, s):
        return jnp.clip(s[0] + t - 3, 0, radial - 1)

    def out(t, s):
        return s[1] + jnp.clip(t - 6, 0, count - 1)

    def one(w, index=0):
        return pl.BlockSpec((1, azimuth, w), lambda t, s: (own(t, s), 0, index))

    def three(w, index=0):
        return pl.BlockSpec((3, 1, azimuth, w), lambda t, s: (0, own(t, s), 0, index))

    def deep(t, s):
        g = s[0] + t - 3
        return jnp.clip(jnp.where(g < 0, g + 3, g - radial), 0, 2)

    def two(t, s):
        g = s[0] + t - 3
        return jnp.clip(jnp.where(g < 0, g + 2, g - radial), 0, 1)

    side = pl.BlockSpec((1, PACKED, width), lambda t, s: (own(t, s), 0, 0))
    parts = []
    if middle:
        ring = width - NPOL
        out_width = ring
        args = [density, velocity, magnetic, *sides]
        specs = [one(width), three(width), three(width), side, side]
    else:
        ring = 2 * NPOL
        out_width = width
        parts = [(first, p.shape[2], p.shape[1]) for first, p in polar]
        polar = [p for _, p in polar]
        args = [density, density, velocity, velocity, magnetic, magnetic, *polar, *sides, *mids]
        specs = [one(NPOL), one(NPOL, tiles - 1), three(NPOL), three(NPOL, tiles - 1),
                 three(NPOL), three(NPOL, tiles - 1)]

        def place(t, s, part):
            first, slots, depth = part
            block = own(t, s) // depth
            return jnp.clip((block - s[2]) * s[3] - first, 0, slots - 1)

        for part in parts:
            specs.append(pl.BlockSpec(
                (4, 1, 1, azimuth + HALO, NPOL),
                lambda t, s, part=part: (0, own(t, s) % part[2], place(t, s, part), 0, 0)))
        specs += [side, side]
        mid_width = width - NPOL
        specs += [pl.BlockSpec((1, azimuth, mid_width), lambda t, s: (out(t, s), 0, 0)),
                  pl.BlockSpec((3, 1, azimuth, mid_width), lambda t, s: (0, out(t, s), 0, 0))]
    used = len(args)
    extra = 0
    if ghosts is not None:
        planes, corner, filtered = ghosts
        where = [lambda t, s: deep(t, s), lambda t, s: 3 + deep(t, s), lambda t, s: 6, lambda t, s: 7]
        index = where + [lambda t, s: 8 + two(t, s), lambda t, s: 10, lambda t, s: 11]
        for f in index:
            args.append(planes)
            specs.append(pl.BlockSpec((1, azimuth, width), lambda t, s, f=f: (f(t, s), 0, 0)))
        for first in (0, 2):
            args.append(corner)
            specs.append(pl.BlockSpec(
                (1, PACKED, width), lambda t, s, first=first: (first + two(t, s), 0, 0)))
        if filtered is not None:
            for f in where:
                args.append(filtered)
                specs.append(pl.BlockSpec(
                    (1, azimuth + HALO, NPOL), lambda t, s, f=f: (f(t, s), 0, 0)))
        extra = len(args) - used
    aliases = {}
    if into is not None:
        for i, x in enumerate(into):
            aliases[1 + len(args)] = i
            args.append(x)
            specs.append(pl.BlockSpec(memory_space=pl.ANY))

    def kernel(starts, *refs):
        ins, outs, scratch = refs[:used], refs[len(args) : len(args) + 2], refs[len(args) + 2 :]
        spare = refs[used : used + extra] if extra else None
        if not middle:
            n = len(polar)
            ins = ins[:6] + (ins[6 : 6 + n],) + ins[6 + n :]
        stencil_kernel(middle, radial, azimuth, parts, starts, ins, spare, outs, scratch)

    rows = FRONT + azimuth + 2 * TILE
    scratch = (
        [pltpu.VMEM((8, rows, ring), jnp.float32)] * 7
        + [pltpu.VMEM((4, rows, ring), jnp.float32)] * 3
        + [pltpu.VMEM((azimuth, ring), jnp.float32)] * 5
    )
    return pl.pallas_call(
        kernel,
        grid_spec=pltpu.PrefetchScalarGridSpec(
            num_scalar_prefetch=1,
            grid=(count + 6,),
            in_specs=specs,
            out_specs=[
                pl.BlockSpec((1, azimuth, out_width), lambda t, s: (out(t, s), 0, 0)),
                pl.BlockSpec((3, 1, azimuth, out_width), lambda t, s: (0, out(t, s), 0, 0)),
            ],
            scratch_shapes=scratch,
        ),
        out_shape=[
            jax.ShapeDtypeStruct((radial, azimuth, out_width), jnp.float32),
            jax.ShapeDtypeStruct((3, radial, azimuth, out_width), jnp.float32),
        ],
        input_output_aliases=aliases,
        compiler_params=pltpu.CompilerParams(
            dimension_semantics=("arbitrary",), vmem_limit_bytes=62 * 1024 * 1024
        ),
        cost_estimate=pl.CostEstimate(
            flops=1000 * count * azimuth * ring, bytes_accessed=48 * count * azimuth * width,
            transcendentals=0,
        ),
        name="section_mid" if middle else "section_polar",
    )(starts, *args)


def swap_rows(x):
    return lax.ppermute(x, "row", [(0, 1), (1, 0)])


def section(density, velocity, magnetic):
    radial, azimuth, width = density.shape
    devices = lax.axis_size("phi")
    pairs = 4 * radial // devices
    depth = radial // pairs
    sent = [(0, pairs - 1), (pairs - 1, 1)] if pairs > 1 else [(0, 1)]
    returned = [(0, 1)]
    if pairs > 2:
        returned.append((1, pairs - 2))
    if pairs > 1:
        returned.append((pairs - 1, 1))
    split = pairs > 1
    low = lax.axis_index("row") == 0
    fields = (density, velocity, magnetic)

    def pick(a, b):
        return jnp.where(low, jnp.int32(a), jnp.int32(b))

    def transpose(x, share, rows):
        x = x.reshape(devices, share, rows, NPOL)
        return lax.all_to_all(x, "phi", split_axis=0, concat_axis=0, tiled=True)

    order = jnp.stack([pick(pairs - 1, 0), pick(-1, 1)])
    packed = [pack_lines(density, velocity, order, a, n, depth) for a, n in sent]
    first_rows, last_rows = pack_sides(density, velocity, magnetic)

    far, near, pair = pick(radial - 3, 0), pick(radial - 1, 0), pick(radial - 2, 0)

    def plane(x, c, n, start, size):
        return lax.dynamic_slice(x, (c, start, 0, 0), (n, size, azimuth, width)).reshape(
            n * size, azimuth, width)

    planes = jnp.concatenate(
        [lax.dynamic_slice_in_dim(density, far, 3, 0), plane(velocity, 0, 1, far, 3),
         plane(velocity, 1, 2, near, 1), plane(magnetic, 0, 1, pair, 2),
         plane(magnetic, 1, 2, near, 1)], axis=0)
    around = [(i, (i + 1) % devices) for i in range(devices)]
    back = [(j, i) for i, j in around]

    side_low = lax.ppermute(last_rows, "phi", around)
    side_high = lax.ppermute(first_rows, "phi", back)
    sides = (side_low, side_high)
    lines = [transpose(packed[0], sent[0][1], azimuth)]
    planes = swap_rows(planes)

    def starts(s):
        return jnp.concatenate([jnp.stack([s, s]), order])

    deep = radial - REACH
    mids = stencil(True, deep, starts(pick(0, REACH)), fields, sides)
    if split:
        packed[1], mids = lax.optimization_barrier((packed[1], tuple(mids)))
        lines.append(transpose(packed[1], sent[1][1], azimuth))
    corner = swap_rows(
        jnp.concatenate([lax.dynamic_slice_in_dim(x, pair, 2, 0) for x in sides], axis=0))

    smooth = [filter_lines(lines[0], a, n, width) for a, n in returned[: max(1, len(returned) - 1)]]
    if split:
        smooth.append(filter_lines(lines[1], 0, 1, width))
    mids = stencil(True, REACH, starts(pick(deep, 0)), fields, sides,
                   ghosts=(planes, corner, None), into=mids)
    polar = []
    for i, (a, n) in enumerate(returned):
        if i + 1 < len(returned):
            smooth[i], smooth[i + 1] = lax.optimization_barrier((smooth[i], smooth[i + 1]))
        elif i > 0:
            smooth[i], mids = lax.optimization_barrier((smooth[i], tuple(mids)))
        back_again = transpose(smooth[i], n, azimuth + HALO)
        polar.append((a, back_again.reshape(4, depth, n, azimuth + HALO, NPOL)))

    first = polar[0][1][:, :, 0]
    far, near = pick(depth - 3, 0), pick(depth - 1, 0)
    ends = lax.dynamic_slice_in_dim(first[:2], far, 3, 1).reshape(6, azimuth + HALO, NPOL)
    close = lax.dynamic_slice_in_dim(first[2:], near, 1, 1).reshape(2, azimuth + HALO, NPOL)
    filtered = swap_rows(jnp.concatenate([ends, close], axis=0))

    edge = depth * sent[0][1] - REACH
    early = polar[:-1] if split else polar
    out = stencil(False, edge, starts(pick(radial - edge, 0)), fields, sides,
                  ghosts=(planes, corner, filtered), polar=early, mids=mids)
    if split:
        late, out = lax.optimization_barrier((polar[-1][1], tuple(out)))
        polar[-1] = (polar[-1][0], late)
    out = stencil(False, radial - edge, starts(pick(0, edge)), fields, sides, polar=polar,
                  mids=mids, into=out)
    return tuple(out)


def solution(mesh):
    placed = (P("row", "phi", None), P(None, "row", "phi", None), P(None, "row", "phi", None))
    return jax.shard_map(
        section,
        mesh=mesh,
        in_specs=placed,
        out_specs=(P("row", "phi", None), P(None, "row", "phi", None)),
        check_vma=False,
    )
```

profile of v0, /device:TPU:0, one launch (start us, length us, event | category | flops | bytes accessed | tf_op | source)
XLA Modules:
  0.0 386.9 jit_solution(15202617252026448772)
XLA Ops:
  0.6 0.6 pad_add_fusion.order
  1.2 5.9 %pack_lines.2 = f32[4,4,3,128,128]{4,3,2,1,0:T(8,128)} custom-call(s32[2]{0:T(128)} %pad_add_fusion.order, f32[16,128,512]{2,1,0:T(8,128)} %refs_1_.9, f32[16,128,512]{2,1,0:T(8,128)} %refs_1_.9, f32[3,16,128,512]{3,2,1,0:T(8,128)} %refs_3_.4, f32[3,16,128,512]{3,2,1,0:T(8,128)} %refs_3_.4), custom_call_target="tpu_custom_call" | custom-call | tf_op jit(solution)/shard_map/pack_lines/pallas_call | solution.py:214
  7.2 7.4 %all-to-all-start = ((f32[16,3,128,128]{3,2,1,0:T(8,128)}), f32[16,3,128,128]{3,2,1,0:T(8,128)}, u32[]{:S(2)}, u32[]{:S(2)}) async-start(f32[16,3,128,128]{3,2,1,0:T(8,128)} %bitcast.28), calls=%async_computation | async-start | bytes 6291456 | tf_op jit(solution)/shard_map/all_to_all | solution.py:707
  14.6 4.0 %pack_sides.1 = (f32[16,16,512]{2,1,0:T(8,128)}, f32[16,16,512]{2,1,0:T(8,128)}) custom-call(f32[16,128,512]{2,1,0:T(8,128)} %refs_1_.9, f32[16,128,512]{2,1,0:T(8,128)} %refs_1_.9, f32[3,16,128,512]{3,2,1,0:T(8,128)} %refs_3_.4, f32[3,16,128,512]{3,2,1,0:T(8,128)} %refs_3_.4, f32[3,16,128,512]{3,2,1,0:T(8,128)} %refs_5_.3, f32[3,16,128,512]{3,2,1,0:T(8,128)} %refs_5_.3), custom_call_target="tpu_custom_call" | custom-call | tf_op jit(solution)/shard_map/pack_sides/pallas_call | solution.py:250
  18.6 0.3 collective-permute-start
  19.0 4.1 %collective-permute-start.1 = (f32[16,16,512]{2,1,0:T(8,128)}, f32[16,16,512]{2,1,0:T(8,128)S(1)}, u32[]{:S(2)}, u32[]{:S(2)}) collective-permute-start(f32[16,16,512]{2,1,0:T(8,128)} %get-tuple-element.26), channel_id=1, source_target_pairs={{1,0},{2,1},{3,2},{4,3},{5,4},{6,5},{7,6},{8,7},{9,8},{10,9},{11,1... | collective-permute-start | bytes 1572872 | tf_op jit(solution)/shard_map/ppermute | solution.py:727
  23.0 3.3 pack_lines.3
  26.4 0.6 add_add_fusion.1.starts
  27.0 49.9 %collective-permute-done.refs_3_.refs_8_.refs_9_ = f32[16,16,512]{2,1,0:T(8,128)S(1)} collective-permute-done((f32[16,16,512]{2,1,0:T(8,128)}, f32[16,16,512]{2,1,0:T(8,128)S(1)}, u32[]{:S(2)}, u32[]{:S(2)}) %collective-permute-start) | collective-permute-done | bytes 524320 | tf_op jit(solution)/shard_map/ppermute | solution.py:726
  76.9 0.0 collective-permute-done.1.refs_4_.refs_9_.refs_10_
  76.9 0.8 copy-done.1
  77.8 0.8 copy-done.2
  78.6 49.5 %section_mid.2 = (f32[16,128,384]{2,1,0:T(8,128)}, f32[3,16,128,384]{3,2,1,0:T(8,128)}) custom-call(s32[4]{0:T(128)} %add_add_fusion.1.starts, f32[16,128,512]{2,1,0:T(8,128)} %refs_1_.9, f32[3,16,128,512]{3,2,1,0:T(8,128)} %refs_3_.4, f32[3,16,128,512]{3,2,1,0:T(8,128)} %refs_5_.3, f32[16,16,512]{2,1,0:T(8,128)} %copy-done.1, f32[16,16,512]{2,1,0:T(8,128)} %copy-done.2), custom_call_target="tpu_custom_call" | custom-call | flops 638976000 | bytes 40894464 | tf_op jit(solution)/shard_map/section_mid/pallas_call | solution.py:655
  128.1 0.0 all-to-all-done.refs_0_.refs_1_
  128.1 17.6 %all-to-all-start.2 = ((f32[16,1,128,128]{3,2,1,0:T(8,128)}), f32[16,1,128,128]{3,2,1,0:T(8,128)S(1)}, u32[]{:S(2)}, u32[]{:S(2)}) async-start(f32[16,1,128,128]{3,2,1,0:T(8,128)} %bitcast.29), calls=%async_computation.2 | async-start | bytes 2097152 | tf_op jit(solution)/shard_map/all_to_all | solution.py:707
  145.6 7.3 %polar_filter.3 = f32[16,1,136,128]{3,2,1,0:T(8,128)} custom-call(f32[16,3,128,128]{3,2,1,0:T(8,128)} %all-to-all-done.refs_0_.refs_1_, f32[9,256,256]{2,1,0:T(8,128)} %constant.35.clone.refs_1_.refs_2_, f32[9,128,128]{2,1,0:T(8,128)} %constant.36.clone.refs_2_.refs_3_), custom_call_target="tpu_custom_call" | custom-call | flops 1073741824 | bytes 6291456 | tf_op jit(solution)/shard_map/polar_filter/pallas_call | solution.py:175
  152.9 9.1 %polar_filter.4 = f32[16,2,136,128]{3,2,1,0:T(8,128)} custom-call(f32[16,3,128,128]{3,2,1,0:T(8,128)} %all-to-all-done.refs_0_.refs_1_, f32[16,3,128,128]{3,2,1,0:T(8,128)} %all-to-all-done.refs_0_.refs_1_, f32[9,256,256]{2,1,0:T(8,128)} %constant.35.clone.refs_1_.refs_2_, f32[9,128,128]{2,1,0:T(8,128)} %constant.36.clone.refs_2_.refs_3_), custom_call_target="tpu_custom_call" | custom-call | flops 2147483648 | bytes 6291456 | tf_op jit(solution)/shard_map/polar_filter/pallas_call | solution.py:175
  161.9 6.6 %all-to-all-done.2.refs_0_ = f32[16,1,128,128]{3,2,1,0:T(8,128)S(1)} async-done(((f32[16,1,128,128]{3,2,1,0:T(8,128)}), f32[16,1,128,128]{3,2,1,0:T(8,128)S(1)}, u32[]{:S(2)}, u32[]{:S(2)}) %all-to-all-start.2) | async-done | bytes 1048608 | tf_op jit(solution)/shard_map/all_to_all | solution.py:707
  168.5 7.0 %all-to-all-start.1 = ((f32[16,1,136,128]{3,2,1,0:T(8,128)}), f32[16,1,136,128]{3,2,1,0:T(8,128)S(1)}, u32[]{:S(2)}, u32[]{:S(2)}) async-start(f32[16,1,136,128]{3,2,1,0:T(8,128)} %polar_filter.3), calls=%async_computation.1 | async-start | bytes 2228224 | tf_op jit(solution)/shard_map/all_to_all | solution.py:707
  175.5 0.0 copy-done.4
  175.5 7.3 %polar_filter.5 = f32[16,1,136,128]{3,2,1,0:T(8,128)} custom-call(f32[16,1,128,128]{3,2,1,0:T(8,128)} %copy-done.4, f32[9,256,256]{2,1,0:T(8,128)} %constant.35.clone.refs_1_.refs_2_, f32[9,128,128]{2,1,0:T(8,128)} %constant.36.clone.refs_2_.refs_3_), custom_call_target="tpu_custom_call" | custom-call | flops 1073741824 | bytes 2097152 | tf_op jit(solution)/shard_map/polar_filter/pallas_call | solution.py:175
  182.8 16.7 %all-to-all-done.1 = f32[16,1,136,128]{3,2,1,0:T(8,128)S(1)} async-done(((f32[16,1,136,128]{3,2,1,0:T(8,128)}), f32[16,1,136,128]{3,2,1,0:T(8,128)S(1)}, u32[]{:S(2)}, u32[]{:S(2)}) %all-to-all-start.1) | async-done | bytes 1114144 | tf_op jit(solution)/shard_map/all_to_all | solution.py:707
  199.4 7.2 %all-to-all-start.3 = ((f32[16,2,136,128]{3,2,1,0:T(8,128)}), f32[16,2,136,128]{3,2,1,0:T(8,128)}, u32[]{:S(2)}, u32[]{:S(2)}) async-start(f32[16,2,136,128]{3,2,1,0:T(8,128)} %polar_filter.4), calls=%async_computation.3 | async-start | bytes 4456448 | tf_op jit(solution)/shard_map/all_to_all | solution.py:707
  206.6 1.2 dynamic-slice_dynamic-update-slice_fusion
  207.8 1.2 bitcast_dynamic-update-slice_fusion
  209.0 1.1 bitcast_dynamic-update-slice_fusion.3
  210.1 1.1 bitcast_dynamic-update-slice_fusion.2
  211.2 1.1 bitcast_dynamic-update-slice_fusion.1
  212.3 2.8 collective-permute-start.2
  215.1 0.8 constant_dynamic-slice_fusion.2
  216.0 0.8 constant_dynamic-slice_fusion.1
  216.8 0.1 collective-permute-start.3
  216.9 0.6 add_add_fusion.2.starts
  217.5 69.0 %collective-permute-done.3.refs_12_.refs_13_.refs_19_.refs_20_ = f32[4,16,512]{2,1,0:T(8,128)S(1)} collective-permute-done((f32[4,16,512]{2,1,0:T(8,128)S(1)}, f32[4,16,512]{2,1,0:T(8,128)S(1)}, u32[]{:S(2)}, u32[]{:S(2)}) %collective-permute-start.3) | collective-permute-done | bytes 131104 | tf_op jit(solution)/shard_map/ppermute | solution.py:684
  286.5 0.0 collective-permute-done.2.refs_5_.refs_6_.refs_7_.refs_8_.refs_9_.refs_10_.refs_11_.refs_12_.refs_13_.refs_14_.refs_15_.refs_16_.refs_17_.refs_18_
  286.5 0.7 copy-done.5
  287.2 19.6 %section_mid.3 = (f32[16,128,384]{2,1,0:T(8,128)}, f32[3,16,128,384]{3,2,1,0:T(8,128)}) custom-call(s32[4]{0:T(128)} %add_add_fusion.2.starts, f32[16,128,512]{2,1,0:T(8,128)} %refs_1_.9, f32[3,16,128,512]{3,2,1,0:T(8,128)} %refs_3_.4, f32[3,16,128,512]{3,2,1,0:T(8,128)} %refs_5_.3, ...), custom_call_target="tpu_custom_call", output_to_operand_aliasing={{0}: (15, {}), {1}: (16, {})} | custom-call | flops 147456000 | bytes 9437184 | tf_op jit(solution)/shard_map/section_mid/pallas_call | solution.py:655
  306.8 0.0 all-to-all-done.3
  306.8 5.8 %all-to-all-start.4 = ((f32[16,1,136,128]{3,2,1,0:T(8,128)}), f32[16,1,136,128]{3,2,1,0:T(8,128)}, u32[]{:S(2)}, u32[]{:S(2)}) async-start(f32[16,1,136,128]{3,2,1,0:T(8,128)} %polar_filter.5), calls=%async_computation.4 | async-start | bytes 2228224 | tf_op jit(solution)/shard_map/all_to_all | solution.py:707
  312.6 0.1 fusion
  312.8 1.5 collective-permute-start.4
  314.3 0.6 add_add_fusion.starts
  314.9 0.7 add_add_fusion.3.starts
  315.6 12.2 %collective-permute-done.4.refs_21_.refs_22_.refs_23_.refs_24_ = f32[8,136,128]{2,1,0:T(8,128)S(1)} collective-permute-done((f32[8,136,128]{2,1,0:T(8,128)S(1)}, f32[8,136,128]{2,1,0:T(8,128)S(1)}, u32[]{:S(2)}, u32[]{:S(2)}) %collective-permute-start.4) | collective-permute-done | bytes 557088 | tf_op jit(solution)/shard_map/ppermute | solution.py:684
  327.7 0.8 copy-done.3
  328.5 32.8 %section_polar.2 = (f32[16,128,512]{2,1,0:T(8,128)}, f32[3,16,128,512]{3,2,1,0:T(8,128)}) custom-call(s32[4]{0:T(128)} %add_add_fusion.3.starts, f32[16,128,512]{2,1,0:T(8,128)} %refs_1_.9, f32[16,128,512]{2,1,0:T(8,128)} %refs_1_.9, f32[3,16,128,512]{3,2,1,0:T(8,128)} %refs_3_.4, f32[3,16,128,512]{3,2,1,0:T(8,128)} %refs_3_.4, f32[3,16,128,512]{3,2,1,0:T(8,128)} %refs_5_.3, ...), custom_call_target="tpu_custom_call" | custom-call | flops 294912000 | bytes 28311552 | tf_op jit(solution)/shard_map/section_polar/pallas_call | solution.py:655
  361.4 0.0 all-to-all-done.4
  361.4 25.3 %section_polar.3 = (f32[16,128,512]{2,1,0:T(8,128)}, f32[3,16,128,512]{3,2,1,0:T(8,128)}) custom-call(s32[4]{0:T(128)} %add_add_fusion.starts, f32[16,128,512]{2,1,0:T(8,128)} %refs_1_.9, f32[16,128,512]{2,1,0:T(8,128)} %refs_1_.9, f32[3,16,128,512]{3,2,1,0:T(8,128)} %refs_3_.4, ...), custom_call_target="tpu_custom_call", output_to_operand_aliasing={{0}: (14, {}), {1}: (15, {})} | custom-call | flops 229376000 | bytes 22020096 | tf_op jit(solution)/shard_map/section_polar/pallas_call | solution.py:655
  (11 shorter events, 0.1 us)
Async XLA Ops:
  7.2 120.9 %all-to-all-start = ((f32[16,3,128,128]{3,2,1,0:T(8,128)}), f32[16,3,128,128]{3,2,1,0:T(8,128)}, u32[]{:S(2)}, u32[]{:S(2)}) async-start(f32[16,3,128,128]{3,2,1,0:T(8,128)} %bitcast.28), calls=%async_computation | async-start | bytes 6291456 | tf_op jit(solution)/shard_map/all_to_all | solution.py:707
  18.6 58.3 %collective-permute-start = (f32[16,16,512]{2,1,0:T(8,128)}, f32[16,16,512]{2,1,0:T(8,128)S(1)}, u32[]{:S(2)}, u32[]{:S(2)}) collective-permute-start(f32[16,16,512]{2,1,0:T(8,128)} %get-tuple-element.25), channel_id=1, source_target_pairs={{0,1},{1,2},{2,3},{3,4},{4,5},{5,6},{6,7},{7,8},{8,9},{9,10},{10,1... | collective-permute-start | bytes 1572872 | tf_op jit(solution)/shard_map/ppermute | solution.py:726
  19.0 58.0 %collective-permute-start.1 = (f32[16,16,512]{2,1,0:T(8,128)}, f32[16,16,512]{2,1,0:T(8,128)S(1)}, u32[]{:S(2)}, u32[]{:S(2)}) collective-permute-start(f32[16,16,512]{2,1,0:T(8,128)} %get-tuple-element.26), channel_id=1, source_target_pairs={{1,0},{2,1},{3,2},{4,3},{5,4},{6,5},{7,6},{8,7},{9,8},{10,9},{11,1... | collective-permute-start | bytes 1572872 | tf_op jit(solution)/shard_map/ppermute | solution.py:727
  76.9 0.8 copy-start.1
  77.8 0.8 copy-start.2
  128.1 40.5 %all-to-all-start.2 = ((f32[16,1,128,128]{3,2,1,0:T(8,128)}), f32[16,1,128,128]{3,2,1,0:T(8,128)S(1)}, u32[]{:S(2)}, u32[]{:S(2)}) async-start(f32[16,1,128,128]{3,2,1,0:T(8,128)} %bitcast.29), calls=%async_computation.2 | async-start | bytes 2097152 | tf_op jit(solution)/shard_map/all_to_all | solution.py:707
  168.5 7.0 %copy-start.4 = (f32[16,1,128,128]{3,2,1,0:T(8,128)}, f32[16,1,128,128]{3,2,1,0:T(8,128)S(1)}, u32[]{:S(2)}) copy-start(f32[16,1,128,128]{3,2,1,0:T(8,128)S(1)} %all-to-all-done.2.refs_0_) | copy-start | bytes 3145732
  168.5 30.9 %all-to-all-start.1 = ((f32[16,1,136,128]{3,2,1,0:T(8,128)}), f32[16,1,136,128]{3,2,1,0:T(8,128)S(1)}, u32[]{:S(2)}, u32[]{:S(2)}) async-start(f32[16,1,136,128]{3,2,1,0:T(8,128)} %polar_filter.3), calls=%async_computation.1 | async-start | bytes 2228224 | tf_op jit(solution)/shard_map/all_to_all | solution.py:707
  199.4 113.1 %copy-start = (f32[16,1,136,128]{3,2,1,0:T(8,128)}, f32[16,1,136,128]{3,2,1,0:T(8,128)S(1)}, u32[]{:S(2)}) copy-start(f32[16,1,136,128]{3,2,1,0:T(8,128)S(1)} %all-to-all-done.1) | copy-start | bytes 3342340
  199.4 107.3 %all-to-all-start.3 = ((f32[16,2,136,128]{3,2,1,0:T(8,128)}), f32[16,2,136,128]{3,2,1,0:T(8,128)}, u32[]{:S(2)}, u32[]{:S(2)}) async-start(f32[16,2,136,128]{3,2,1,0:T(8,128)} %polar_filter.4), calls=%async_computation.3 | async-start | bytes 4456448 | tf_op jit(solution)/shard_map/all_to_all | solution.py:707
  212.3 74.2 %collective-permute-start.2 = (f32[12,128,512]{2,1,0:T(8,128)S(1)}, f32[12,128,512]{2,1,0:T(8,128)}, u32[]{:S(2)}, u32[]{:S(2)}) collective-permute-start(f32[12,128,512]{2,1,0:T(8,128)S(1)} %bitcast_dynamic-update-slice_fusion.1), channel_id=1, source_target_pairs={{0,16},{16,0},{1,17},{17,1},{2,18},{18,2},{3,19},{19,3},{4,20},{20... | collective-permute-start | bytes 9437192 | tf_op jit(solution)/shard_map/ppermute | solution.py:684
  216.8 69.7 %collective-permute-start.3 = (f32[4,16,512]{2,1,0:T(8,128)S(1)}, f32[4,16,512]{2,1,0:T(8,128)S(1)}, u32[]{:S(2)}, u32[]{:S(2)}) collective-permute-start(f32[4,16,512]{2,1,0:T(8,128)S(1)} %pad_maximum_fusion.1), channel_id=1, source_target_pairs={{0,16},{16,0},{1,17},{17,1},{2,18},{18,2},{3,19},{19,3},{4,20},{20... | collective-permute-start | bytes 393224 | tf_op jit(solution)/shard_map/ppermute | solution.py:684
  286.5 0.7 copy-start.5
  306.8 54.6 %all-to-all-start.4 = ((f32[16,1,136,128]{3,2,1,0:T(8,128)}), f32[16,1,136,128]{3,2,1,0:T(8,128)}, u32[]{:S(2)}, u32[]{:S(2)}) async-start(f32[16,1,136,128]{3,2,1,0:T(8,128)} %polar_filter.5), calls=%async_computation.4 | async-start | bytes 2228224 | tf_op jit(solution)/shard_map/all_to_all | solution.py:707
  312.8 15.0 %collective-permute-start.4 = (f32[8,136,128]{2,1,0:T(8,128)S(1)}, f32[8,136,128]{2,1,0:T(8,128)S(1)}, u32[]{:S(2)}, u32[]{:S(2)}) collective-permute-start(f32[8,136,128]{2,1,0:T(8,128)S(1)} %pad_maximum_fusion), channel_id=1, source_target_pairs={{0,16},{16,0},{1,17},{17,1},{2,18},{18,2},{3,19},{19,3},{4,20},{20... | collective-permute-start | bytes 1671176 | tf_op jit(solution)/shard_map/ppermute | solution.py:684
  327.7 0.8 copy-start.3
where the time goes:
time: 388 us; the launch traced here: 387 us
  Pallas kernels  164 us (42%)
  waiting for transfers between devices  154 us (40%)
  starting transfers between devices  53.8 us (14%)
  local copies, waits for them, and re-layouts  10.6 us (3%)
    pallas_call x4, Pallas kernels, stencil(): pl.pallas_call(kernel, grid_spec=pltpu.PrefetchScalarGridSpec(num_scalar_...  127 us
    ppermute x3, waiting for transfers between devices, swap_rows(): return lax.ppermute(x, 'row', [(0, 1), (1, 0)])  81.2 us
    ppermute x1, waiting for transfers between devices, section(): side_low = lax.ppermute(last_rows, 'phi', around)  49.9 us
    all_to_all x5, starting transfers between devices, transpose(): return lax.all_to_all(x, 'phi', split_axis=0, concat_axis=0, tiled=True)  44.9 us
    pallas_call x3, Pallas kernels, filter_lines(): pl.pallas_call(lambda *refs: filter_kernel(group, inner, blocks, *refs),...  23.6 us
    all_to_all x5, waiting for transfers between devices, transpose(): return lax.all_to_all(x, 'phi', split_axis=0, concat_axis=0, tiled=True)  23.2 us
    pallas_call x2, Pallas kernels, pack_lines(): pl.pallas_call(kernel, grid_spec=pltpu.PrefetchScalarGridSpec(num_scalar_...  9.27 us
  transfers between devices with their start and end apart: 10, of which 5 were waited for; matrix products, arithmetic and copies ran while one was open for 3% of the time, Pallas kernels for 34%

commit v1 on v0

--- a/solution.py
+++ b/solution.py
@@ -99,22 +99,22 @@
     k2 = np.arange(RADIX // 2 + 1)[:, None]
     mode = k2 + RADIX * np.arange(inner)[None, :]
     angle = 2.0 * np.pi / cells * ((mode[:, :, None] * np.arange(inner)) % cells)
-    cos, sin = np.cos(angle), np.sin(angle)
-    forward = np.concatenate(
-        [np.concatenate([cos, sin], 2), np.concatenate([-sin, cos], 2)], 1
-    ).astype(np.float32)
+    waves = np.concatenate([np.cos(angle), np.sin(angle)], 2).astype(np.float32)
     rows = np.arange(NPOL)
     theta = np.where(rows < half_polar, rows, theta_count - NPOL + rows)
     row_square = np.sin(np.pi * (theta + 0.5) / theta_count) ** 2
     edge = np.sin(np.pi * (half_polar + 0.5) / theta_count)
     mode_square = (edge * np.sin(np.pi * mode / cells)) ** 2
-    damping = row_square / np.maximum(row_square, mode_square[:, :, None])
-    return forward, (damping / cells).astype(np.float32)
+    return (
+        waves,
+        np.broadcast_to(row_square, (TILE, NPOL)).astype(np.float32),
+        np.ascontiguousarray(mode_square.T).astype(np.float32),
+    )
 
 
 def filter_kernel(group, inner, blocks, *refs):
     x_refs = refs[:group]
-    basis_ref, damp_ref, out_ref = refs[group:]
+    waves_ref, row_ref, mode_ref, out_ref = refs[group:]
     devices, _, azimuth, _ = x_refs[0].shape
 
     def slab(d):
@@ -126,7 +126,10 @@
     spectrum = real_fft([slab(d) for d in range(RADIX)])
     filtered = []
     for k, (re, im) in enumerate(spectrum):
-        basis = basis_ref[k]
+        waves = waves_ref[k]
+        cos, sin = waves[:, :inner], waves[:, inner:]
+        turned = jnp.concatenate([-sin, cos], axis=1)
+        basis = jnp.concatenate([waves, turned], axis=0)
         if im is None:
             forward = basis[:, :inner]
             stacked = re
@@ -136,7 +139,9 @@
         modes = jnp.dot(
             forward, stacked, precision=lax.Precision.HIGHEST, preferred_element_type=jnp.float32
         )
-        damp = damp_ref[k]
+        row_square = row_ref[0:1, :]
+        damp = row_square / jnp.maximum(row_square, mode_ref[:, k : k + 1])
+        damp = damp * (1.0 / (inner * RADIX))
         damp = jnp.concatenate([damp, damp], axis=0)
         if group > 1:
             damp = jnp.concatenate([damp] * group, axis=1)
@@ -166,7 +171,7 @@
     cells = devices * azimuth
     inner = cells // RADIX
     blocks = inner // azimuth
-    forward, damping = filter_tables(cells, theta_count)
+    tables = filter_tables(cells, theta_count)
 
     def slot(g):
         return pl.BlockSpec((devices, 1, azimuth, NPOL), lambda p: (0, first + g, 0, 0))
@@ -176,10 +181,7 @@
         lambda *refs: filter_kernel(group, inner, blocks, *refs),
         grid=(1,),
         in_specs=[slot(g) for g in range(group)]
-        + [
-            pl.BlockSpec(forward.shape, lambda p: (0, 0, 0)),
-            pl.BlockSpec(damping.shape, lambda p: (0, 0, 0)),
-        ],
+        + [pl.BlockSpec(x.shape, lambda p, n=x.ndim: (0,) * n) for x in tables],
         out_specs=pl.BlockSpec(shape, lambda p: (0, 0, 0, 0)),
         out_shape=jax.ShapeDtypeStruct(shape, jnp.float32),
         compiler_params=pltpu.CompilerParams(vmem_limit_bytes=56 * 1024 * 1024),
@@ -187,7 +189,7 @@
             flops=32 * inner * cells * NPOL * group, bytes_accessed=8 * lines.size, transcendentals=0
         ),
         name="polar_filter",
-    )(*[lines] * group, jnp.asarray(forward), jnp.asarray(damping))
+    )(*[lines] * group, *[jnp.asarray(x) for x in tables])
 
 
 def pack_lines(density, velocity, order, first, slots, depth):
@@ -195,29 +197,33 @@
     half = NPOL // 2
     last = width // NPOL - 1
 
+    cut = 2 if depth % 2 == 0 else 1
+    step = depth // cut
+
     def kernel(order, d0, d1, v0, v1, out):
         lane = lax.broadcasted_iota(jnp.int32, (azimuth, NPOL), 1)
-        for i in range(depth):
+        for i in range(step):
             out[0, i, 0] = jnp.where(lane < half, d0[i], d1[i])
             for c in range(3):
                 out[1 + c, i, 0] = jnp.where(lane < half, v0[c, i], v1[c, i])
 
-    def block(t, s):
-        return s[0] + (first + t) * s[1]
+    def block(t, h, s):
+        return (s[0] + (first + t) * s[1]) * cut + h
 
     def dens(tile):
-        return pl.BlockSpec((depth, azimuth, NPOL), lambda t, s: (block(t, s), 0, tile))
+        return pl.BlockSpec((step, azimuth, NPOL), lambda t, h, s: (block(t, h, s), 0, tile))
 
     def vel(tile):
-        return pl.BlockSpec((3, depth, azimuth, NPOL), lambda t, s: (0, block(t, s), 0, tile))
+        return pl.BlockSpec((3, step, azimuth, NPOL), lambda t, h, s: (0, block(t, h, s), 0, tile))
 
     return pl.pallas_call(
         kernel,
         grid_spec=pltpu.PrefetchScalarGridSpec(
             num_scalar_prefetch=1,
-            grid=(slots,),
+            grid=(slots, cut),
             in_specs=[dens(0), dens(last), vel(0), vel(last)],
-            out_specs=pl.BlockSpec((4, depth, 1, azimuth, NPOL), lambda t, s: (0, 0, t, 0, 0)),
+            out_specs=pl.BlockSpec(
+                (4, step, 1, azimuth, NPOL), lambda t, h, s: (0, h, t, 0, 0)),
         ),
         out_shape=jax.ShapeDtypeStruct((4, depth, slots, azimuth, NPOL), jnp.float32),
         name="pack_lines",

time: 388 us -> 389 us (level)
  no operation moved by 1% of the time
where the time goes in v1:
time: 389 us; the launch traced here: 387 us
  Pallas kernels  163 us (42%)
  waiting for transfers between devices  156 us (40%)
  starting transfers between devices  53.6 us (14%)
  local copies, waits for them, and re-layouts  10.6 us (3%)
    pallas_call x4, Pallas kernels, stencil(): pl.pallas_call(kernel, grid_spec=pltpu.PrefetchScalarGridSpec(num_scalar_...  127 us
    ppermute x3, waiting for transfers between devices, swap_rows(): return lax.ppermute(x, 'row', [(0, 1), (1, 0)])  81.2 us
    ppermute x1, waiting for transfers between devices, section(): side_low = lax.ppermute(last_rows, 'phi', around)  50.1 us
    all_to_all x5, starting transfers between devices, transpose(): return lax.all_to_all(x, 'phi', split_axis=0, concat_axis=0, tiled=True)  44.7 us
    all_to_all x5, waiting for transfers between devices, transpose(): return lax.all_to_all(x, 'phi', split_axis=0, concat_axis=0, tiled=True)  24.7 us
    pallas_call x3, Pallas kernels, filter_lines(): pl.pallas_call(lambda *refs: filter_kernel(group, inner, blocks, *refs),...  22.2 us
    pallas_call x2, Pallas kernels, pack_lines(): pl.pallas_call(kernel, grid_spec=pltpu.PrefetchScalarGridSpec(num_scalar_...  9.86 us
  transfers between devices with their start and end apart: 10, of which 5 were waited for; matrix products, arithmetic and copies ran while one was open for 3% of the time, Pallas kernels for 34%

profile of v1, /device:TPU:0, one launch (start us, length us, event | category | flops | bytes accessed | tf_op | source)
XLA Modules:
  0.0 387.5 jit_solution(12100512910715600993)
XLA Ops:
  0.6 0.6 pad_add_fusion.order
  1.2 6.7 %pack_lines.2 = f32[4,4,3,128,128]{4,3,2,1,0:T(8,128)} custom-call(s32[2]{0:T(128)} %pad_add_fusion.order, f32[16,128,512]{2,1,0:T(8,128)} %refs_1_.9, f32[16,128,512]{2,1,0:T(8,128)} %refs_1_.9, f32[3,16,128,512]{3,2,1,0:T(8,128)} %refs_3_.6, f32[3,16,128,512]{3,2,1,0:T(8,128)} %refs_3_.6), custom_call_target="tpu_custom_call" | custom-call | tf_op jit(solution)/shard_map/pack_lines/pallas_call | solution.py:219
  7.9 7.4 %all-to-all-start = ((f32[16,3,128,128]{3,2,1,0:T(8,128)}), f32[16,3,128,128]{3,2,1,0:T(8,128)}, u32[]{:S(2)}, u32[]{:S(2)}) async-start(f32[16,3,128,128]{3,2,1,0:T(8,128)} %bitcast.28), calls=%async_computation | async-start | bytes 6291456 | tf_op jit(solution)/shard_map/all_to_all | solution.py:713
  15.4 4.0 %pack_sides.1 = (f32[16,16,512]{2,1,0:T(8,128)}, f32[16,16,512]{2,1,0:T(8,128)}) custom-call(f32[16,128,512]{2,1,0:T(8,128)} %refs_1_.9, f32[16,128,512]{2,1,0:T(8,128)} %refs_1_.9, f32[3,16,128,512]{3,2,1,0:T(8,128)} %refs_3_.6, f32[3,16,128,512]{3,2,1,0:T(8,128)} %refs_3_.6, f32[3,16,128,512]{3,2,1,0:T(8,128)} %refs_5_.3, f32[3,16,128,512]{3,2,1,0:T(8,128)} %refs_5_.3), custom_call_target="tpu_custom_call" | custom-call | tf_op jit(solution)/shard_map/pack_sides/pallas_call | solution.py:256
  19.4 0.3 collective-permute-start
  19.7 4.1 %collective-permute-start.1 = (f32[16,16,512]{2,1,0:T(8,128)}, f32[16,16,512]{2,1,0:T(8,128)S(1)}, u32[]{:S(2)}, u32[]{:S(2)}) collective-permute-start(f32[16,16,512]{2,1,0:T(8,128)} %get-tuple-element.26), channel_id=1, source_target_pairs={{1,0},{2,1},{3,2},{4,3},{5,4},{6,5},{7,6},{8,7},{9,8},{10,9},{11,1... | collective-permute-start | bytes 1572872 | tf_op jit(solution)/shard_map/ppermute | solution.py:733
  23.8 3.2 pack_lines.3
  27.0 0.6 add_add_fusion.1.starts
  27.6 50.1 %collective-permute-done.refs_3_.refs_8_.refs_9_ = f32[16,16,512]{2,1,0:T(8,128)S(1)} collective-permute-done((f32[16,16,512]{2,1,0:T(8,128)}, f32[16,16,512]{2,1,0:T(8,128)S(1)}, u32[]{:S(2)}, u32[]{:S(2)}) %collective-permute-start) | collective-permute-done | bytes 524320 | tf_op jit(solution)/shard_map/ppermute | solution.py:732
  77.7 0.0 collective-permute-done.1.refs_4_.refs_9_.refs_10_
  77.7 0.8 copy-done.1
  78.5 0.8 copy-done.2
  79.3 49.5 %section_mid.2 = (f32[16,128,384]{2,1,0:T(8,128)}, f32[3,16,128,384]{3,2,1,0:T(8,128)}) custom-call(s32[4]{0:T(128)} %add_add_fusion.1.starts, f32[16,128,512]{2,1,0:T(8,128)} %refs_1_.9, f32[3,16,128,512]{3,2,1,0:T(8,128)} %refs_3_.6, f32[3,16,128,512]{3,2,1,0:T(8,128)} %refs_5_.3, f32[16,16,512]{2,1,0:T(8,128)} %copy-done.1, f32[16,16,512]{2,1,0:T(8,128)} %copy-done.2), custom_call_target="tpu_custom_call" | custom-call | flops 638976000 | bytes 40894464 | tf_op jit(solution)/shard_map/section_mid/pallas_call | solution.py:661
  128.8 0.0 all-to-all-done.refs_0_.refs_1_
  128.8 17.6 %all-to-all-start.2 = ((f32[16,1,128,128]{3,2,1,0:T(8,128)}), f32[16,1,128,128]{3,2,1,0:T(8,128)S(1)}, u32[]{:S(2)}, u32[]{:S(2)}) async-start(f32[16,1,128,128]{3,2,1,0:T(8,128)} %bitcast.29), calls=%async_computation.2 | async-start | bytes 2097152 | tf_op jit(solution)/shard_map/all_to_all | solution.py:713
  146.4 6.8 %polar_filter.3 = f32[16,1,136,128]{3,2,1,0:T(8,128)} custom-call(f32[16,3,128,128]{3,2,1,0:T(8,128)} %all-to-all-done.refs_0_.refs_1_, f32[9,128,256]{2,1,0:T(8,128)} %constant.37.clone.refs_1_.refs_2_, f32[8,128]{1,0:T(8,128)} %constant.38.clone.refs_2_.refs_3_, f32[128,9]{1,0:T(8,128)} %constant.39.clone.refs_3_.refs_4_), custom_call_target="tpu_custom_call" | custom-call | flops 1073741824 | bytes 6291456 | tf_op jit(solution)/shard_map/polar_filter/pallas_call | solution.py:180
  153.1 8.6 %polar_filter.4 = f32[16,2,136,128]{3,2,1,0:T(8,128)} custom-call(f32[16,3,128,128]{3,2,1,0:T(8,128)} %all-to-all-done.refs_0_.refs_1_, f32[16,3,128,128]{3,2,1,0:T(8,128)} %all-to-all-done.refs_0_.refs_1_, f32[9,128,256]{2,1,0:T(8,128)} %constant.37.clone.refs_1_.refs_2_, f32[8,128]{1,0:T(8,128)} %constant.38.clone.refs_2_.refs_3_, ...), custom_call_target="tpu_custom_call" | custom-call | flops 2147483648 | bytes 6291456 | tf_op jit(solution)/shard_map/polar_filter/pallas_call | solution.py:180
  161.8 7.5 %all-to-all-done.2.refs_0_ = f32[16,1,128,128]{3,2,1,0:T(8,128)S(1)} async-done(((f32[16,1,128,128]{3,2,1,0:T(8,128)}), f32[16,1,128,128]{3,2,1,0:T(8,128)S(1)}, u32[]{:S(2)}, u32[]{:S(2)}) %all-to-all-start.2) | async-done | bytes 1048608 | tf_op jit(solution)/shard_map/all_to_all | solution.py:713
  169.3 6.8 %all-to-all-start.1 = ((f32[16,1,136,128]{3,2,1,0:T(8,128)}), f32[16,1,136,128]{3,2,1,0:T(8,128)S(1)}, u32[]{:S(2)}, u32[]{:S(2)}) async-start(f32[16,1,136,128]{3,2,1,0:T(8,128)} %polar_filter.3), calls=%async_computation.1 | async-start | bytes 2228224 | tf_op jit(solution)/shard_map/all_to_all | solution.py:713
  176.1 0.0 copy-done.5
  176.1 6.8 %polar_filter.5 = f32[16,1,136,128]{3,2,1,0:T(8,128)} custom-call(f32[16,1,128,128]{3,2,1,0:T(8,128)} %copy-done.5, f32[9,128,256]{2,1,0:T(8,128)} %constant.37.clone.refs_1_.refs_2_, f32[8,128]{1,0:T(8,128)} %constant.38.clone.refs_2_.refs_3_, f32[128,9]{1,0:T(8,128)} %constant.39.clone.refs_3_.refs_4_), custom_call_target="tpu_custom_call" | custom-call | flops 1073741824 | bytes 2097152 | tf_op jit(solution)/shard_map/polar_filter/pallas_call | solution.py:180
  182.9 17.2 %all-to-all-done.1 = f32[16,1,136,128]{3,2,1,0:T(8,128)S(1)} async-done(((f32[16,1,136,128]{3,2,1,0:T(8,128)}), f32[16,1,136,128]{3,2,1,0:T(8,128)S(1)}, u32[]{:S(2)}, u32[]{:S(2)}) %all-to-all-start.1) | async-done | bytes 1114144 | tf_op jit(solution)/shard_map/all_to_all | solution.py:713
  200.0 7.2 %all-to-all-start.3 = ((f32[16,2,136,128]{3,2,1,0:T(8,128)}), f32[16,2,136,128]{3,2,1,0:T(8,128)}, u32[]{:S(2)}, u32[]{:S(2)}) async-start(f32[16,2,136,128]{3,2,1,0:T(8,128)} %polar_filter.4), calls=%async_computation.3 | async-start | bytes 4456448 | tf_op jit(solution)/shard_map/all_to_all | solution.py:713
  207.2 1.2 dynamic-slice_dynamic-update-slice_fusion
  208.4 1.2 bitcast_dynamic-update-slice_fusion
  209.6 1.1 bitcast_dynamic-update-slice_fusion.3
  210.7 1.1 bitcast_dynamic-update-slice_fusion.2
  211.8 1.1 bitcast_dynamic-update-slice_fusion.1
  212.9 2.8 collective-permute-start.2
  215.7 0.8 constant_dynamic-slice_fusion.2
  216.5 0.8 constant_dynamic-slice_fusion.1
  217.4 0.1 collective-permute-start.3
  217.5 0.6 add_add_fusion.2.starts
  218.1 69.0 %collective-permute-done.3.refs_12_.refs_13_.refs_19_.refs_20_ = f32[4,16,512]{2,1,0:T(8,128)S(1)} collective-permute-done((f32[4,16,512]{2,1,0:T(8,128)S(1)}, f32[4,16,512]{2,1,0:T(8,128)S(1)}, u32[]{:S(2)}, u32[]{:S(2)}) %collective-permute-start.3) | collective-permute-done | bytes 131104 | tf_op jit(solution)/shard_map/ppermute | solution.py:690
  287.1 0.0 collective-permute-done.2.refs_5_.refs_6_.refs_7_.refs_8_.refs_9_.refs_10_.refs_11_.refs_12_.refs_13_.refs_14_.refs_15_.refs_16_.refs_17_.refs_18_
  287.1 0.7 copy-done.4
  287.8 19.6 %section_mid.3 = (f32[16,128,384]{2,1,0:T(8,128)}, f32[3,16,128,384]{3,2,1,0:T(8,128)}) custom-call(s32[4]{0:T(128)} %add_add_fusion.2.starts, f32[16,128,512]{2,1,0:T(8,128)} %refs_1_.9, f32[3,16,128,512]{3,2,1,0:T(8,128)} %refs_3_.6, f32[3,16,128,512]{3,2,1,0:T(8,128)} %refs_5_.3, ...), custom_call_target="tpu_custom_call", output_to_operand_aliasing={{0}: (15, {}), {1}: (16, {})} | custom-call | flops 147456000 | bytes 9437184 | tf_op jit(solution)/shard_map/section_mid/pallas_call | solution.py:661
  307.4 0.0 all-to-all-done.3
  307.4 5.8 %all-to-all-start.4 = ((f32[16,1,136,128]{3,2,1,0:T(8,128)}), f32[16,1,136,128]{3,2,1,0:T(8,128)}, u32[]{:S(2)}, u32[]{:S(2)}) async-start(f32[16,1,136,128]{3,2,1,0:T(8,128)} %polar_filter.5), calls=%async_computation.4 | async-start | bytes 2228224 | tf_op jit(solution)/shard_map/all_to_all | solution.py:713
  313.2 0.1 fusion
  313.4 1.5 collective-permute-start.4
  314.9 0.6 add_add_fusion.starts
  315.5 0.7 add_add_fusion.3.starts
  316.1 12.2 %collective-permute-done.4.refs_21_.refs_22_.refs_23_.refs_24_ = f32[8,136,128]{2,1,0:T(8,128)S(1)} collective-permute-done((f32[8,136,128]{2,1,0:T(8,128)S(1)}, f32[8,136,128]{2,1,0:T(8,128)S(1)}, u32[]{:S(2)}, u32[]{:S(2)}) %collective-permute-start.4) | collective-permute-done | bytes 557088 | tf_op jit(solution)/shard_map/ppermute | solution.py:690
  328.3 0.8 copy-done.3
  329.1 32.8 %section_polar.2 = (f32[16,128,512]{2,1,0:T(8,128)}, f32[3,16,128,512]{3,2,1,0:T(8,128)}) custom-call(s32[4]{0:T(128)} %add_add_fusion.3.starts, f32[16,128,512]{2,1,0:T(8,128)} %refs_1_.9, f32[16,128,512]{2,1,0:T(8,128)} %refs_1_.9, f32[3,16,128,512]{3,2,1,0:T(8,128)} %refs_3_.6, f32[3,16,128,512]{3,2,1,0:T(8,128)} %refs_3_.6, f32[3,16,128,512]{3,2,1,0:T(8,128)} %refs_5_.3, ...), custom_call_target="tpu_custom_call" | custom-call | flops 294912000 | bytes 28311552 | tf_op jit(solution)/shard_map/section_polar/pallas_call | solution.py:661
  362.0 0.0 all-to-all-done.4
  362.0 25.3 %section_polar.3 = (f32[16,128,512]{2,1,0:T(8,128)}, f32[3,16,128,512]{3,2,1,0:T(8,128)}) custom-call(s32[4]{0:T(128)} %add_add_fusion.starts, f32[16,128,512]{2,1,0:T(8,128)} %refs_1_.9, f32[16,128,512]{2,1,0:T(8,128)} %refs_1_.9, f32[3,16,128,512]{3,2,1,0:T(8,128)} %refs_3_.6, ...), custom_call_target="tpu_custom_call", output_to_operand_aliasing={{0}: (14, {}), {1}: (15, {})} | custom-call | flops 229376000 | bytes 22020096 | tf_op jit(solution)/shard_map/section_polar/pallas_call | solution.py:661
  (11 shorter events, 0.1 us)
Async XLA Ops:
  7.9 120.9 %all-to-all-start = ((f32[16,3,128,128]{3,2,1,0:T(8,128)}), f32[16,3,128,128]{3,2,1,0:T(8,128)}, u32[]{:S(2)}, u32[]{:S(2)}) async-start(f32[16,3,128,128]{3,2,1,0:T(8,128)} %bitcast.28), calls=%async_computation | async-start | bytes 6291456 | tf_op jit(solution)/shard_map/all_to_all | solution.py:713
  19.4 58.3 %collective-permute-start = (f32[16,16,512]{2,1,0:T(8,128)}, f32[16,16,512]{2,1,0:T(8,128)S(1)}, u32[]{:S(2)}, u32[]{:S(2)}) collective-permute-start(f32[16,16,512]{2,1,0:T(8,128)} %get-tuple-element.25), channel_id=1, source_target_pairs={{0,1},{1,2},{2,3},{3,4},{4,5},{5,6},{6,7},{7,8},{8,9},{9,10},{10,1... | collective-permute-start | bytes 1572872 | tf_op jit(solution)/shard_map/ppermute | solution.py:732
  19.7 58.0 %collective-permute-start.1 = (f32[16,16,512]{2,1,0:T(8,128)}, f32[16,16,512]{2,1,0:T(8,128)S(1)}, u32[]{:S(2)}, u32[]{:S(2)}) collective-permute-start(f32[16,16,512]{2,1,0:T(8,128)} %get-tuple-element.26), channel_id=1, source_target_pairs={{1,0},{2,1},{3,2},{4,3},{5,4},{6,5},{7,6},{8,7},{9,8},{10,9},{11,1... | collective-permute-start | bytes 1572872 | tf_op jit(solution)/shard_map/ppermute | solution.py:733
  77.7 0.8 copy-start.1
  78.5 0.8 copy-start.2
  128.8 40.5 %all-to-all-start.2 = ((f32[16,1,128,128]{3,2,1,0:T(8,128)}), f32[16,1,128,128]{3,2,1,0:T(8,128)S(1)}, u32[]{:S(2)}, u32[]{:S(2)}) async-start(f32[16,1,128,128]{3,2,1,0:T(8,128)} %bitcast.29), calls=%async_computation.2 | async-start | bytes 2097152 | tf_op jit(solution)/shard_map/all_to_all | solution.py:713
  169.3 6.8 %copy-start.5 = (f32[16,1,128,128]{3,2,1,0:T(8,128)}, f32[16,1,128,128]{3,2,1,0:T(8,128)S(1)}, u32[]{:S(2)}) copy-start(f32[16,1,128,128]{3,2,1,0:T(8,128)S(1)} %all-to-all-done.2.refs_0_) | copy-start | bytes 3145732
  169.3 30.7 %all-to-all-start.1 = ((f32[16,1,136,128]{3,2,1,0:T(8,128)}), f32[16,1,136,128]{3,2,1,0:T(8,128)S(1)}, u32[]{:S(2)}, u32[]{:S(2)}) async-start(f32[16,1,136,128]{3,2,1,0:T(8,128)} %polar_filter.3), calls=%async_computation.1 | async-start | bytes 2228224 | tf_op jit(solution)/shard_map/all_to_all | solution.py:713
  200.0 113.1 %copy-start = (f32[16,1,136,128]{3,2,1,0:T(8,128)}, f32[16,1,136,128]{3,2,1,0:T(8,128)S(1)}, u32[]{:S(2)}) copy-start(f32[16,1,136,128]{3,2,1,0:T(8,128)S(1)} %all-to-all-done.1) | copy-start | bytes 3342340
  200.0 107.3 %all-to-all-start.3 = ((f32[16,2,136,128]{3,2,1,0:T(8,128)}), f32[16,2,136,128]{3,2,1,0:T(8,128)}, u32[]{:S(2)}, u32[]{:S(2)}) async-start(f32[16,2,136,128]{3,2,1,0:T(8,128)} %polar_filter.4), calls=%async_computation.3 | async-start | bytes 4456448 | tf_op jit(solution)/shard_map/all_to_all | solution.py:713
  212.9 74.2 %collective-permute-start.2 = (f32[12,128,512]{2,1,0:T(8,128)S(1)}, f32[12,128,512]{2,1,0:T(8,128)}, u32[]{:S(2)}, u32[]{:S(2)}) collective-permute-start(f32[12,128,512]{2,1,0:T(8,128)S(1)} %bitcast_dynamic-update-slice_fusion.1), channel_id=1, source_target_pairs={{0,16},{16,0},{1,17},{17,1},{2,18},{18,2},{3,19},{19,3},{4,20},{20... | collective-permute-start | bytes 9437192 | tf_op jit(solution)/shard_map/ppermute | solution.py:690
  217.4 69.7 %collective-permute-start.3 = (f32[4,16,512]{2,1,0:T(8,128)S(1)}, f32[4,16,512]{2,1,0:T(8,128)S(1)}, u32[]{:S(2)}, u32[]{:S(2)}) collective-permute-start(f32[4,16,512]{2,1,0:T(8,128)S(1)} %pad_maximum_fusion.1), channel_id=1, source_target_pairs={{0,16},{16,0},{1,17},{17,1},{2,18},{18,2},{3,19},{19,3},{4,20},{20... | collective-permute-start | bytes 393224 | tf_op jit(solution)/shard_map/ppermute | solution.py:690
  287.1 0.7 copy-start.4
  307.4 54.6 %all-to-all-start.4 = ((f32[16,1,136,128]{3,2,1,0:T(8,128)}), f32[16,1,136,128]{3,2,1,0:T(8,128)}, u32[]{:S(2)}, u32[]{:S(2)}) async-start(f32[16,1,136,128]{3,2,1,0:T(8,128)} %polar_filter.5), calls=%async_computation.4 | async-start | bytes 2228224 | tf_op jit(solution)/shard_map/all_to_all | solution.py:713
  313.4 15.0 %collective-permute-start.4 = (f32[8,136,128]{2,1,0:T(8,128)S(1)}, f32[8,136,128]{2,1,0:T(8,128)S(1)}, u32[]{:S(2)}, u32[]{:S(2)}) collective-permute-start(f32[8,136,128]{2,1,0:T(8,128)S(1)} %pad_maximum_fusion), channel_id=1, source_target_pairs={{0,16},{16,0},{1,17},{17,1},{2,18},{18,2},{3,19},{19,3},{4,20},{20... | collective-permute-start | bytes 1671176 | tf_op jit(solution)/shard_map/ppermute | solution.py:690
  328.3 0.8 copy-start.3
